TPU v7x, 128 devices: a whole 4x4x4 slice. The times are simulated.
128 devices in a mesh: row: 16 (over z, x), col: 8 (over y, core).
Axes of the slice: x: 4, y: 4, z: 4, core: 2. Of those that a mesh axis runs over, the one named last changes fastest.
Arguments:
- density_first: bfloat16 [12288, 12288], P('row', 'col'), may hold values from -0.0068359375 to 0.0068359375
- density_second: bfloat16 [12288, 12288], P('row', 'col'), may hold values from -0.0068359375 to 0.0068359375
- basis: bfloat16 [256, 4096, 896], P(('row', 'col')), may hold values from -6 to 6
- tile_list: int32 [256, 7], P(('row', 'col')), may hold values from 0 to 95, as said below
- tile_count: int32 [256], P(('row', 'col')), may hold values from 5 to 7, as said below
- point_count: int32 [256], P(('row', 'col')), may hold values from 1024 to 4096, as said below
- offsets: float32 [3, 256, 4096], P(None, ('row', 'col')), may hold values from -5 to 5
- weights: float32 [256, 4096], P(('row', 'col')), may hold values from 0.05 to 1
- atom_of_point: int32 [256, 4096], P(('row', 'col')), may hold values from 0 to 1023, as said below
Outputs:
- density: float32 [2, 256, 4096], P(None, ('row', 'col'))
- moments: float32 [2, 9, 1024], replicated
Inputs may be any that keep to these rules, and one draw needn't show every extreme that they name: `tile_list`: the 7 tile numbers of each batch are 7 consecutive numbers in some order. `tile_count`: some batch has 7. `point_count`: some batch has 4096. `atom_of_point`: the points of batch g belong to atoms (g * 4 + j) mod 1024 with j from 0 to 7.
All inputs are finite; a program needn't handle non-finite values.
Results may differ from a plain program's by a relative error of at most 0.0003.
Values may be sent and summed in bfloat16 or wider, within the bound.
A program may use at most 192 MiB of HBM per device.

v0:
```python
import functools

import jax
import jax.numpy as jnp
from jax import lax
from jax.experimental import pallas as pl
from jax.experimental.pallas import tpu as pltpu
from jax.sharding import Mesh
from jax.sharding import PartitionSpec as P

TILE = 128
ATOMS = 1024
ROW = ("row_0", "row_1")
COL = ("col_0", "col_1")
ROW_COL = ("row_0", "row_1", "col_0", "col_1")
KT = 7
N_ROW = 16
N_COL = 8
DEVS = N_ROW * N_COL
NT = 96
STARTS = NT - KT + 1
LOCAL_T = NT // N_ROW
LOCAL_U = NT // N_COL
BLOCK = 512
GROUPS = BLOCK // TILE
F32 = jnp.float32
BF16 = jnp.bfloat16
I16 = jnp.int16
I32 = jnp.int32
VMEM_LIMIT = 60 * 1024 * 1024
MESH_ID = pl.DeviceIdType.MESH
SMEM_SPEC = pl.BlockSpec(memory_space=pltpu.SMEM)
VMEM_SPEC = pl.BlockSpec(memory_space=pltpu.VMEM)
ANY_SPEC = pl.BlockSpec(memory_space=pl.ANY)


def encode(value):
    size = jnp.abs(value)
    safe = jnp.maximum(size, 2.0**-38)
    power = jnp.floor(jnp.log2(safe))
    code = (power + 37.0) * 1024.0 + safe * jnp.exp2(10.0 - power)
    code = jnp.clip(jnp.floor(code + 0.5), 0.0, 32767.0)
    code = jnp.where(size >= 2.0**-38, code, 0.0)
    code = jnp.where(value < 0.0, -code, code)
    return code.astype(I32).astype(I16)


def decode(code):
    code = code.astype(I32)
    size = jnp.abs(code)
    power = lax.shift_right_logical(size, 10).astype(F32)
    fraction = (lax.bitwise_and(size, 1023) + 1024).astype(F32)
    value = fraction * jnp.exp2(power - 48.0)
    value = jnp.where(size > 0, value, 0.0)
    return jnp.where(code < 0, -value, value)


def harmonics(x, y, z):
    radius_sq = x * x + y * y + z * z
    return [
        None,
        x,
        y,
        z,
        x * y,
        y * z,
        3.0 * z * z - radius_sq,
        x * z,
        x * x - y * y,
    ]


CHUNKS = ((0, 0, 4), (0, 4, 7), (1, 0, 4), (1, 4, 6), (1, 6, 7))
OTHERS = pl.ds(0, DEVS - 1)


def flat(spot):
    return ((spot[0] * 4 + spot[1]) * 4 + spot[2]) * 2 + spot[3]


def wait_all(ref, sem):
    pltpu.make_async_copy(ref, ref, sem).wait()


def to_everyone(spot, send):
    z, x, y, core = spot
    way = 1 - 2 * core
    zs = [(z + way * k + 4) % 4 for k in range(4)]
    xs = [(x + way * k + 4) % 4 for k in range(4)]
    first = tuple((y + way * k + 4) % 4 for k in range(4))
    both = [core, 1 - core]
    for turn in range(2):

        def step(i, ys, turn=turn):
            for n in range(16):
                b = n % 4
                a = (n // 4 + b) % 4
                partner = (zs[a], xs[b], ys[(a + b) % 4], both[(turn + a) % 2])
                if n == 0 and turn == 0:

                    @pl.when(i > 0)
                    def _(partner=partner):
                        send(partner)
                else:
                    send(partner)
            return (*ys[1:], ys[0])

        lax.fori_loop(0, 4, step, first)


def remote(source, target, send_sem, recv_sem, partner):
    pltpu.make_async_remote_copy(
        src_ref=source,
        dst_ref=target,
        send_sem=send_sem,
        recv_sem=recv_sem,
        device_id=partner,
        device_id_type=MESH_ID,
    ).start()


def extract_tile(r, e, tile, m, ul, t):
    row_tile = r + 16 * t
    if ul == 0:
        d = e
        near = 1 - e // 4
        key = row_tile + d * (1 - near)
        turned = (e >= 1) & (e <= 3)
    else:
        d = 8 - e
        near = (e + 3) // 8
        key = row_tile - d * near
        turned = e <= 4
    kind = near * d + (1 - near) * (7 - d)
    q = (kind + 4 * m + (key + 16) // 16 + 15) % 8
    value = tile.astype(F32)
    value = jnp.where(turned, value.T, value)
    return q, value.reshape(N_ROW, 8, TILE).astype(BF16)


def whole_kernel(
    first,
    second,
    basis,
    tile_list,
    tile_count,
    point_count,
    far_offsets,
    far_weights,
    far_atoms,
    density,
    moments,
    offsets,
    weights,
    atoms,
    tiles,
    banded,
    slices,
    table,
    windows,
    own_starts,
    vector_starts,
    starts,
    outgoing,
    matrix,
    kept,
    geometry,
    labels,
    dens,
    sums,
    own_moments,
    all_moments,
    point_sems,
    tile_sems,
    basis_sems,
    here_sems,
    send_sems,
    recv_sems,
    *buffers,
):
    arrived = buffers[: len(CHUNKS)]
    values = buffers[len(CHUNKS) :]
    spot = [lax.axis_index(name) for name in ROW_COL]
    me = flat(spot)
    r = spot[0] * 4 + spot[1]
    c = spot[2] * 2 + spot[3]
    e = (c - r + 16) % 8
    points = basis.shape[1]
    rows = points // TILE
    point_copies = [
        pltpu.make_async_copy(source, target, point_sems.at[k])
        for k, (source, target) in enumerate(
            [(far_offsets, offsets), (far_weights, weights), (far_atoms, atoms)]
        )
    ]

    def tile_copy(m, ul, t):
        column = (r + 16 * t + e - 8 * ul - c + 64) // 8 - 8
        column = jnp.minimum(jnp.maximum(column, 0), LOCAL_U - 1)
        source = (first, second)[m]
        return pltpu.make_async_copy(
            source.at[pl.ds(t * TILE, TILE), pl.ds(pl.multiple_of(column * TILE, TILE), TILE)],
            tiles.at[m, ul, t],
            tile_sems.at[m, ul, t],
        )

    def basis_copy(b, j):
        return pltpu.make_async_copy(
            basis.at[b, :, pl.ds(j * TILE, TILE)], values[b].at[j], basis_sems.at[b, j]
        )

    todo = [(m, ul, t) for m in range(2) for ul in range(2) for t in range(LOCAL_T)]
    for item in todo:
        tile_copy(*item).start()
    for copy in point_copies:
        copy.start()
    barrier = pltpu.get_barrier_semaphore()
    to_everyone(
        spot,
        lambda partner: pl.semaphore_signal(
            barrier, inc=1, device_id=partner, device_id_type=MESH_ID
        ),
    )

    listed = [[tile_list[b, p] for p in range(KT)] for b in range(2)]
    begin = [functools.reduce(jnp.minimum, one) for one in listed]
    place = [
        [
            jnp.minimum(
                sum(jnp.where(listed[b][p] == begin[b] + t, p, 0) for p in range(KT)), KT - 1
            )
            for t in range(KT)
        ]
        for b in range(2)
    ]
    live = [[(place[b][t] < tile_count[b]).astype(F32) for t in range(KT)] for b in range(2)]
    lane = lax.broadcasted_iota(I32, (1, TILE), 1)
    own_starts[...] = jnp.where(lane == 0, begin[0], begin[1])

    banded[...] = jnp.zeros(banded.shape, BF16)
    for m, ul, t in todo:
        tile_copy(m, ul, t).wait()
        q, value = extract_tile(r, e, tiles[m, ul, t], m, ul, t)
        banded[:, q, ul, m] = value
    pl.semaphore_wait(barrier, DEVS - 1)

    for ul in range(2):

        @pl.when((e <= 6) if ul == 0 else (e >= 2))
        def _(ul=ul):
            to_everyone(
                spot,
                lambda to: remote(
                    banded.at[to[0] * 4 + to[1], to[2] * 2 + to[3], ul],
                    slices.at[me, ul],
                    send_sems.at[1 + ul],
                    recv_sems.at[1 + ul],
                    to,
                ),
            )

    to_everyone(
        spot,
        lambda to: remote(
            own_starts, vector_starts.at[me], send_sems.at[0], recv_sems.at[0], to
        ),
    )
    vector_starts[me] = own_starts[...]
    slices[me] = banded[r, c]
    for b in range(2):
        for j in range(KT):
            basis_copy(b, j).start()
    for copy in point_copies:
        copy.wait()
    for b in range(2):
        for i in range(rows):
            lanes = pl.ds(i * TILE, TILE)
            for k in range(3):
                geometry[k, b, pl.ds(i, 1), :] = offsets[k, pl.ds(b, 1), lanes]
            geometry[3, b, pl.ds(i, 1), :] = weights[pl.ds(b, 1), lanes]
            labels[b, pl.ds(i, 1), :] = atoms[pl.ds(b, 1), lanes]
    wait_all(vector_starts.at[OTHERS], recv_sems.at[0])
    scalars = pltpu.make_async_copy(vector_starts, starts, here_sems.at[0])
    scalars.start()
    scalars.wait()
    for ul in range(2):
        senders = (112, 96)[ul]
        takes_part = (e <= 6) if ul == 0 else (e >= 2)

        @pl.when(takes_part)
        def _(ul=ul, senders=senders):
            wait_all(slices.at[pl.ds(0, senders - 1), ul], recv_sems.at[1 + ul])

        @pl.when(jnp.logical_not(takes_part))
        def _(ul=ul, senders=senders):
            wait_all(slices.at[pl.ds(0, senders), ul], recv_sems.at[1 + ul])

    def kind_of(k):
        return lax.bitwise_and(c - lax.shift_right_logical(k, 4), 7)

    def owner(row_tile, col_tile):
        return lax.bitwise_and(row_tile, 15) * 8 + lax.bitwise_and(col_tile, 7)

    def fill(k, carry):
        which = kind_of(k)
        kind = lax.bitwise_and(which, 3)
        m = lax.shift_right_logical(which, 2)
        far = k + kind
        paired = lax.shift_right_logical(kind + 3, 2)
        upper = slices[owner(k, far), 0, m].astype(F32)
        lower = slices[owner(far, k), paired, m].astype(F32)
        table[2 * k] = encode(upper + lower * paired.astype(F32))
        near = k + 9 + kind + (1 - paired)
        upper = slices[owner(near, k), 0, m].astype(F32)
        lower = slices[owner(k, near + 8), 1, m].astype(F32)
        table[2 * k + 1] = encode(upper + lower)
        return carry

    lax.fori_loop(0, NT, fill, 0, unroll=8)

    def window(a, carry):
        for t in range(KT):
            kind = lax.bitwise_and(kind_of(a + t), 3)
            wraps = lax.shift_right_logical(t + kind + 1, 3)
            windows[a, t] = table[2 * (a + t) + wraps]
        return carry

    lax.fori_loop(0, STARTS, window, 0, unroll=5)

    for b in range(2):

        def pack(d, carry, b=b):
            outgoing[b, d] = windows[starts[d, 0, b]]
            return carry

        lax.fori_loop(0, DEVS, pack, 0, unroll=8)

    for n, (b, low, high) in enumerate(CHUNKS):
        part = pl.ds(low, high - low)
        to_everyone(
            spot,
            lambda to, n=n, b=b, part=part: remote(
                outgoing.at[b, flat(to), part],
                arrived[n].at[me],
                send_sems.at[3 + n],
                recv_sems.at[3 + n],
                to,
            ),
        )
        arrived[n][me] = outgoing[b, me, part]

    spots = lax.broadcasted_iota(I32, (rows, TILE), 0) * TILE + lax.broadcasted_iota(
        I32, (rows, TILE), 1
    )
    for n, (b, low, high) in enumerate(CHUNKS):
        begins = low == 0
        ends = high == KT
        if begins:
            for j in range(KT):
                basis_copy(b, j).wait()
        wait_all(arrived[n].at[OTHERS], recv_sems.at[3 + n])
        for t in range(low, high):
            turn = lax.shift_right_arithmetic(begin[b] + t, 4)
            for kind in range(4):
                alive = live[b][t] * live[b][(t + kind) % KT]
                for m in range(2):
                    q = lax.bitwise_and(kind + 4 * m + turn, 7)
                    codes = [arrived[n][s * N_COL + q, t - low] for s in range(N_ROW)]
                    value = decode(jnp.concatenate(codes, axis=0)) * alive
                    upper = value.astype(BF16)
                    lower = (value - upper.astype(F32)).astype(BF16)
                    columns = pl.ds(m * TILE, TILE)
                    matrix[t, pl.ds(kind * TILE, TILE), columns] = upper
                    matrix[t, pl.ds((4 + kind) * TILE, TILE), columns] = lower

        def step(block, carry, b=b, low=low, high=high, begins=begins, ends=ends):
            span = pl.ds(pl.multiple_of(block * BLOCK, BLOCK), BLOCK)
            total = None if begins else kept[span, :]
            for t in range(low, high):
                left = jnp.concatenate(
                    [values[b][place[b][(t + i) % KT], span, :] for i in range(4)], axis=1
                )
                product = jnp.dot(
                    left, matrix[t, pl.ds(0, 4 * TILE), :], preferred_element_type=F32
                ) + jnp.dot(
                    left, matrix[t, pl.ds(4 * TILE, 4 * TILE), :], preferred_element_type=F32
                )
                own = left[:, :TILE].astype(F32)
                term = product * jnp.concatenate([own, own], axis=1)
                total = term if total is None else total + term
            if not ends:
                kept[span, :] = total
            else:
                for m in range(2):
                    for i in range(GROUPS):
                        part = total[i * TILE : (i + 1) * TILE, m * TILE : (m + 1) * TILE]
                        dens[m, b, pl.ds(block * GROUPS + i, 1), :] = jnp.sum(
                            part.T, axis=0, keepdims=True
                        )
            return carry

        lax.fori_loop(0, points // BLOCK, step, 0)
        if not ends:
            continue
        inside = spots < point_count[b]
        harmonic = harmonics(geometry[0, b], geometry[1, b], geometry[2, b])
        weight = geometry[3, b]
        factors = [weight] + [weight * item for item in harmonic[1:]]
        base = (me * 8 + b * 4) % ATOMS
        hits = [labels[b] == (base + j) % ATOMS for j in range(8)]
        if b == 0:
            sums[...] = jnp.zeros(sums.shape, F32)
        for m in range(2):
            value = jnp.where(inside, dens[m, b], 0.0)
            dens[m, b] = value
            for h in range(9):
                term = value * factors[h]
                for j in range(8):
                    line = jnp.sum(jnp.where(hits[j], term, 0.0), axis=0, keepdims=True)
                    at = pl.ds((j + 4 * b) * 18 + m * 9 + h, 1)
                    sums[at, :] = line if b == 0 or j >= 4 else sums[at, :] + line
    for i in range(2):
        part = sums[pl.ds(i * TILE, TILE), :]
        own_moments[pl.ds(i, 1), :] = jnp.sum(part.T, axis=0, keepdims=True)
    for m in range(2):
        for b in range(2):
            for i in range(rows):
                density[m, pl.ds(b, 1), pl.ds(i * TILE, TILE)] = dens[m, b, pl.ds(i, 1), :]
    last = 3 + len(CHUNKS)
    to_everyone(
        spot,
        lambda to: remote(
            own_moments, all_moments.at[me], send_sems.at[last], recv_sems.at[last], to
        ),
    )
    all_moments[me] = own_moments[...]
    wait_all(vector_starts.at[OTHERS], send_sems.at[0])
    for ul in range(2):

        @pl.when((e <= 6) if ul == 0 else (e >= 2))
        def _(ul=ul):
            wait_all(slices.at[OTHERS, ul], send_sems.at[1 + ul])

    for n in range(len(CHUNKS)):
        wait_all(arrived[n].at[OTHERS], send_sems.at[3 + n])
    wait_all(all_moments.at[OTHERS], send_sems.at[last])
    wait_all(all_moments.at[OTHERS], recv_sems.at[last])
    moments[...] = all_moments[...]


def whole(first, second, basis, tile_list, tile_count, point_count, offsets, weights, atoms):
    points = basis.shape[1]
    rows = points // TILE
    count = 4 + len(CHUNKS)
    return pl.pallas_call(
        whole_kernel,
        name="whole",
        out_shape=(
            jax.ShapeDtypeStruct((2, 2, points), F32),
            jax.ShapeDtypeStruct((DEVS, 2, TILE), F32),
        ),
        in_specs=[ANY_SPEC] * 3 + [SMEM_SPEC] * 3 + [ANY_SPEC] * 3,
        out_specs=(VMEM_SPEC, VMEM_SPEC),
        scratch_shapes=[
            pltpu.VMEM(offsets.shape, F32),
            pltpu.VMEM(weights.shape, F32),
            pltpu.VMEM(atoms.shape, I32),
            pltpu.VMEM((2, 2, LOCAL_T, TILE, TILE), BF16),
            pltpu.VMEM((N_ROW, N_COL, 2, 2, 8, TILE), BF16),
            pltpu.VMEM((DEVS, 2, 2, 8, TILE), BF16),
            pltpu.VMEM((2 * NT, 8, TILE), I16),
            pltpu.VMEM((STARTS, KT, 8, TILE), I16),
            pltpu.VMEM((1, TILE), I32),
            pltpu.VMEM((DEVS, 1, TILE), I32),
            pltpu.SMEM((DEVS, 1, TILE), I32),
            pltpu.VMEM((2, DEVS, KT, 8, TILE), I16),
            pltpu.VMEM((KT, 8 * TILE, 2 * TILE), BF16),
            pltpu.VMEM((points, 2 * TILE), F32),
            pltpu.VMEM((4, 2, rows, TILE), F32),
            pltpu.VMEM((2, rows, TILE), I32),
            pltpu.VMEM((2, 2, rows, TILE), F32),
            pltpu.VMEM((2 * TILE, TILE), F32),
            pltpu.VMEM((2, TILE), F32),
            pltpu.VMEM((DEVS, 2, TILE), F32),
            pltpu.SemaphoreType.DMA((3,)),
            pltpu.SemaphoreType.DMA((2, 2, LOCAL_T)),
            pltpu.SemaphoreType.DMA((2, KT)),
            pltpu.SemaphoreType.DMA((1,)),
            pltpu.SemaphoreType.DMA((count,)),
            pltpu.SemaphoreType.DMA((count,)),
            *(pltpu.VMEM((DEVS, high - low, 8, TILE), I16) for _, low, high in CHUNKS),
            pltpu.VMEM((KT, points, TILE), BF16),
            pltpu.VMEM((KT, points, TILE), BF16),
        ],
        compiler_params=pltpu.CompilerParams(
            collective_id=0, has_side_effects=True, vmem_limit_bytes=VMEM_LIMIT
        ),
    )(first, second, basis, tile_list, tile_count, point_count, offsets, weights, atoms)


def local(
    density_first,
    density_second,
    basis,
    tile_list,
    tile_count,
    point_count,
    offsets,
    weights,
    atom_of_point,
):
    density, shared = whole(
        density_first,
        density_second,
        basis,
        tile_list,
        tile_count,
        point_count,
        offsets,
        weights,
        atom_of_point,
    )
    everyone = shared.reshape(DEVS, 2 * TILE)
    half = 4 * 18
    main = everyone[:, : 2 * half]
    extra = jnp.roll(everyone[:, 2 * half : 3 * half], 1, axis=0)
    whole_moments = main + jnp.concatenate([extra, jnp.zeros_like(extra)], axis=1)
    return (density, whole_moments.reshape(ATOMS, 18).T.reshape(2, 9, ATOMS))


def solution(mesh):
    torus = Mesh(mesh.devices.reshape(4, 4, 4, 2), ("row_0", "row_1", "col_0", "col_1"))
    in_specs = (
        P(ROW, COL),
        P(ROW, COL),
        P(ROW_COL, None, None),
        P(ROW_COL, None),
        P(ROW_COL),
        P(ROW_COL),
        P(None, ROW_COL, None),
        P(ROW_COL, None),
        P(ROW_COL, None),
    )
    out_specs = (P(None, ROW_COL, None), P())
    return jax.shard_map(local, mesh=torus, in_specs=in_specs, out_specs=out_specs, check_vma=False)
```

profile of v0, /device:TPU:1, one launch (start us, length us, event | category | flops | bytes accessed | tf_op | source)
XLA Modules:
  0.0 109.8 jit_solution(7666429052673356235)
XLA Ops:
  0.6 106.3 %whole.1 = (f32[2,2,4096]{2,1,0:T(2,128)}, f32[128,2,128]{2,1,0:T(2,128)}) custom-call(bf16[768,1536]{1,0:T(8,128)(2,1)} %first.1, bf16[768,1536]{1,0:T(8,128)(2,1)} %second.1, bf16[2,4096,896]{2,1,0:T(8,128)(2,1)} %basis.1, s32[2,7]{1,0:T(2,128)} %tile_list.1, s32[2]{0:T(128)} %tile_count.1, s32[2]{0:T(128)} %point_count.1, f32[3,2,4096]{2,1,0:T(2,128)} %far_offsets.1, ...), custom_call_target="tpu_custom_call" | custom-call | tf_op jit(solution)/shard_map/whole/pallas_call | solution.py:455
  107.0 0.0 copy-start
  107.0 0.9 copy.15
  107.9 0.1 slice.18
  108.0 0.1 slice.19
  108.1 0.2 reshape.14
  108.3 0.2 copy.11
  108.5 0.7 copy.12
  109.2 0.0 copy-done
  109.2 0.6 copy.17
  (2 shorter events, 0.0 us)
Async XLA Ops:
  107.0 2.3 %copy-start = (f32[2,2,4096]{2,1,0:T(2,128)S(1)}, f32[2,2,4096]{2,1,0:T(2,128)}, u32[]{:S(2)}) copy-start(f32[2,2,4096]{2,1,0:T(2,128)} %get-tuple-element.10) | copy-start | bytes 196612
where the time goes:
time: 110 us
  Pallas kernels  106 us (96%)
  local copies, waits for them, and re-layouts  2.83 us (3%)
    pallas_call x1, Pallas kernels, whole(): pl.pallas_call(whole_kernel, name='whole', out_shape=(jax.ShapeDtypeStruc...  106 us
    unnamed x5, local copies, waits for them, and re-layouts  2.27 us

commit v1 on v0

--- a/solution.py
+++ b/solution.py
@@ -21,12 +21,16 @@
 STARTS = NT - KT + 1
 LOCAL_T = NT // N_ROW
 LOCAL_U = NT // N_COL
-BLOCK = 512
+BLOCK = 1024
 GROUPS = BLOCK // TILE
 F32 = jnp.float32
 BF16 = jnp.bfloat16
 I16 = jnp.int16
 I32 = jnp.int32
+F8 = jnp.float8_e5m2
+LOW_SCALE = 2.0**30
+BASIS_SCALE = 2.0**13
+LOW_UNSCALE = 2.0**-43
 VMEM_LIMIT = 60 * 1024 * 1024
 MESH_ID = pl.DeviceIdType.MESH
 SMEM_SPEC = pl.BlockSpec(memory_space=pltpu.SMEM)
@@ -163,6 +167,7 @@
     starts,
     outgoing,
     matrix,
+    low_matrix,
     kept,
     geometry,
     labels,
@@ -179,7 +184,8 @@
     *buffers,
 ):
     arrived = buffers[: len(CHUNKS)]
-    values = buffers[len(CHUNKS) :]
+    values = buffers[len(CHUNKS) : len(CHUNKS) + 2]
+    low_values = buffers[len(CHUNKS) + 2 :]
     spot = [lax.axis_index(name) for name in ROW_COL]
     me = flat(spot)
     r = spot[0] * 4 + spot[1]
@@ -355,9 +361,18 @@
     for n, (b, low, high) in enumerate(CHUNKS):
         begins = low == 0
         ends = high == KT
-        if begins:
-            for j in range(KT):
-                basis_copy(b, j).wait()
+        if n == 0:
+            for each in range(2):
+                for j in range(KT):
+                    basis_copy(each, j).wait()
+
+                    def narrow(i, carry, each=each, j=j):
+                        span = pl.ds(pl.multiple_of(i * BLOCK, BLOCK), BLOCK)
+                        value = values[each][j, span, :].astype(F32) * BASIS_SCALE
+                        low_values[each][j, span, :] = value.astype(F8)
+                        return carry
+
+                    lax.fori_loop(0, points // BLOCK, narrow, 0)
         wait_all(arrived[n].at[OTHERS], recv_sems.at[3 + n])
         for t in range(low, high):
             turn = lax.shift_right_arithmetic(begin[b] + t, 4)
@@ -368,23 +383,21 @@
                     codes = [arrived[n][s * N_COL + q, t - low] for s in range(N_ROW)]
                     value = decode(jnp.concatenate(codes, axis=0)) * alive
                     upper = value.astype(BF16)
-                    lower = (value - upper.astype(F32)).astype(BF16)
+                    lower = (value - upper.astype(F32)) * LOW_SCALE
                     columns = pl.ds(m * TILE, TILE)
                     matrix[t, pl.ds(kind * TILE, TILE), columns] = upper
-                    matrix[t, pl.ds((4 + kind) * TILE, TILE), columns] = lower
+                    low_matrix[t, pl.ds(kind * TILE, TILE), columns] = lower.astype(F8)
 
         def step(block, carry, b=b, low=low, high=high, begins=begins, ends=ends):
             span = pl.ds(pl.multiple_of(block * BLOCK, BLOCK), BLOCK)
             total = None if begins else kept[span, :]
             for t in range(low, high):
-                left = jnp.concatenate(
-                    [values[b][place[b][(t + i) % KT], span, :] for i in range(4)], axis=1
-                )
-                product = jnp.dot(
-                    left, matrix[t, pl.ds(0, 4 * TILE), :], preferred_element_type=F32
-                ) + jnp.dot(
-                    left, matrix[t, pl.ds(4 * TILE, 4 * TILE), :], preferred_element_type=F32
-                )
+                order = [place[b][(t + i) % KT] for i in range(4)]
+                left = jnp.concatenate([values[b][p, span, :] for p in order], axis=1)
+                low_left = jnp.concatenate([low_values[b][p, span, :] for p in order], axis=1)
+                product = jnp.dot(left, matrix[t], preferred_element_type=F32)
+                low = jnp.dot(low_left, low_matrix[t], preferred_element_type=F32)
+                product = product + low * LOW_UNSCALE
                 own = left[:, :TILE].astype(F32)
                 term = product * jnp.concatenate([own, own], axis=1)
                 total = term if total is None else total + term
@@ -474,7 +487,8 @@
             pltpu.VMEM((DEVS, 1, TILE), I32),
             pltpu.SMEM((DEVS, 1, TILE), I32),
             pltpu.VMEM((2, DEVS, KT, 8, TILE), I16),
-            pltpu.VMEM((KT, 8 * TILE, 2 * TILE), BF16),
+            pltpu.VMEM((KT, 4 * TILE, 2 * TILE), BF16),
+            pltpu.VMEM((KT, 4 * TILE, 2 * TILE), F8),
             pltpu.VMEM((points, 2 * TILE), F32),
             pltpu.VMEM((4, 2, rows, TILE), F32),
             pltpu.VMEM((2, rows, TILE), I32),
@@ -491,6 +505,8 @@
             *(pltpu.VMEM((DEVS, high - low, 8, TILE), I16) for _, low, high in CHUNKS),
             pltpu.VMEM((KT, points, TILE), BF16),
             pltpu.VMEM((KT, points, TILE), BF16),
+            pltpu.VMEM((KT, points, TILE), F8),
+            pltpu.VMEM((KT, points, TILE), F8),
         ],
         compiler_params=pltpu.CompilerParams(
             collective_id=0, has_side_effects=True, vmem_limit_bytes=VMEM_LIMIT

time: 110 us -> 100 us (0.909)
  Pallas kernels: 106 us -> 96.6 us
    pallas_call x1, Pallas kernels: 106 us -> 96.6 us  [whole(): pl.pallas_call(whole_kernel, name='whole', out_shape=(jax.ShapeDtypeStruc...]
where the time goes in v1:
time: 100 us
  Pallas kernels  96.6 us (97%)
  local copies, waits for them, and re-layouts  2.83 us (3%)
    pallas_call x1, Pallas kernels, whole(): pl.pallas_call(whole_kernel, name='whole', out_shape=(jax.ShapeDtypeStruc...  96.6 us
    unnamed x5, local copies, waits for them, and re-layouts  2.27 us

profile of v1, /device:TPU:1, one launch (start us, length us, event | category | flops | bytes accessed | tf_op | source)
XLA Modules:
  0.0 100.1 jit_solution(6708241342396065793)
XLA Ops:
  0.6 96.6 %whole.1 = (f32[2,2,4096]{2,1,0:T(2,128)}, f32[128,2,128]{2,1,0:T(2,128)}) custom-call(bf16[768,1536]{1,0:T(8,128)(2,1)} %first.1, bf16[768,1536]{1,0:T(8,128)(2,1)} %second.1, bf16[2,4096,896]{2,1,0:T(8,128)(2,1)} %basis.1, s32[2,7]{1,0:T(2,128)} %tile_list.1, s32[2]{0:T(128)} %tile_count.1, s32[2]{0:T(128)} %point_count.1, f32[3,2,4096]{2,1,0:T(2,128)} %far_offsets.1, ...), custom_call_target="tpu_custom_call" | custom-call | tf_op jit(solution)/shard_map/whole/pallas_call | solution.py:468
  97.2 0.0 copy-start
  97.2 0.9 copy.15
  98.2 0.1 slice.18
  98.3 0.1 slice.19
  98.4 0.2 reshape.14
  98.6 0.2 copy.11
  98.8 0.7 copy.12
  99.5 0.0 copy-done
  99.5 0.6 copy.17
  (2 shorter events, 0.0 us)
Async XLA Ops:
  97.2 2.3 %copy-start = (f32[2,2,4096]{2,1,0:T(2,128)S(1)}, f32[2,2,4096]{2,1,0:T(2,128)}, u32[]{:S(2)}) copy-start(f32[2,2,4096]{2,1,0:T(2,128)} %get-tuple-element.10) | copy-start | bytes 196612

commit v2 on v1

--- a/solution.py
+++ b/solution.py
@@ -21,7 +21,7 @@
 STARTS = NT - KT + 1
 LOCAL_T = NT // N_ROW
 LOCAL_U = NT // N_COL
-BLOCK = 1024
+BLOCK = 2048
 GROUPS = BLOCK // TILE
 F32 = jnp.float32
 BF16 = jnp.bfloat16

time: 100 us -> 99.6 us (level)
  no operation moved by 1% of the time
where the time goes in v2:
time: 99.6 us; the launch traced here: 99.5 us
  Pallas kernels  95.9 us (96%)
  local copies, waits for them, and re-layouts  2.83 us (3%)
    pallas_call x1, Pallas kernels, whole(): pl.pallas_call(whole_kernel, name='whole', out_shape=(jax.ShapeDtypeStruc...  95.9 us
    unnamed x5, local copies, waits for them, and re-layouts  2.27 us

profile of v2, /device:TPU:1, one launch (start us, length us, event | category | flops | bytes accessed | tf_op | source)
XLA Modules:
  0.0 99.5 jit_solution(1455546569500146007)
XLA Ops:
  0.6 95.9 %whole.1 = (f32[2,2,4096]{2,1,0:T(2,128)}, f32[128,2,128]{2,1,0:T(2,128)}) custom-call(bf16[768,1536]{1,0:T(8,128)(2,1)} %first.1, bf16[768,1536]{1,0:T(8,128)(2,1)} %second.1, bf16[2,4096,896]{2,1,0:T(8,128)(2,1)} %basis.1, s32[2,7]{1,0:T(2,128)} %tile_list.1, s32[2]{0:T(128)} %tile_count.1, s32[2]{0:T(128)} %point_count.1, f32[3,2,4096]{2,1,0:T(2,128)} %far_offsets.1, ...), custom_call_target="tpu_custom_call" | custom-call | tf_op jit(solution)/shard_map/whole/pallas_call | solution.py:468
  96.6 0.0 copy-start
  96.6 0.9 copy.15
  97.5 0.1 slice.18
  97.6 0.1 slice.19
  97.7 0.2 reshape.14
  97.9 0.2 copy.11
  98.1 0.7 copy.12
  98.8 0.0 copy-done
  98.8 0.6 copy.17
  (2 shorter events, 0.0 us)
Async XLA Ops:
  96.6 2.3 %copy-start = (f32[2,2,4096]{2,1,0:T(2,128)S(1)}, f32[2,2,4096]{2,1,0:T(2,128)}, u32[]{:S(2)}) copy-start(f32[2,2,4096]{2,1,0:T(2,128)} %get-tuple-element.10) | copy-start | bytes 196612
